TPU v7x, 256 devices: a whole 4x4x8 slice. The times are simulated.
256 devices in a mesh: dp: 8 (over z), expert: 32 (over y, x, core).
Axes of the slice: x: 4, y: 4, z: 8, core: 2. Of those that a mesh axis runs over, the one named last changes fastest.
Arguments:
- tokens: bfloat16 [65536, 1280], P(('dp', 'expert')), may hold values from -14 to 14
- ln_gain: float32 [1280], replicated, may hold values from 0.25 to 1.75
- router: bfloat16 [1280, 32], replicated, may hold values from -0.3125 to 0.3125
- w_in: bfloat16 [32, 5120, 1280], P('expert', 'dp'), may hold values from -0.15625 to 0.15625
- b_in: bfloat16 [32, 5120], P('expert', 'dp'), may hold values from -3 to 3
- w_out: bfloat16 [32, 5120, 1280], P('expert', 'dp'), may hold values from -0.078125 to 0.078125
- b_out: bfloat16 [32, 1280], P('expert'), may hold values from -3 to 3
- expert_choice: int32 [65536], P(('dp', 'expert')), may hold values from 0 to 31
- modality: int32 [65536], P(('dp', 'expert')), may hold values from 0 to 1, as said below
- slot: int32 [65536], P(('dp', 'expert')), may hold values from -1 to 15, as said below
Outputs:
- moe_out: bfloat16 [65536, 1280], P(('dp', 'expert'))
- aux_losses: float32 [2, 2], replicated
Inputs may be any that keep to these rules, and one draw needn't show every extreme that they name: Each source's tokens with one expert and a slot other than -1 have distinct slots, numbered from 0 in token order; one expert has all 16 slots filled in every source. `modality`: every source holds tokens of both modalities.
All inputs are finite; a program needn't handle non-finite values.
Results may differ from a plain program's by a relative error of at most 0.007.
Values may be sent and summed in bfloat16 or wider, within the bound.
A program may use at most 128 MiB of HBM per device.

v0:
```python
import functools
import jax
import jax.numpy as jnp
from jax import lax
from jax.sharding import Mesh
from jax.sharding import PartitionSpec as P

CAP = 16
EXPERT = ("expert_0", "expert_1", "expert_2")
DP_EXPERT = ("dp", "expert_0", "expert_1", "expert_2")


def by_axis(x, axes):
    return functools.reduce(lax.psum, axes, x)


def layer_norm(tokens, ln_gain):
    values = tokens.astype(jnp.float32)
    center = values - jnp.mean(values, axis=-1, keepdims=True)
    spread = jnp.mean(center * center, axis=-1, keepdims=True)
    return (center * lax.rsqrt(spread + 1e-06) * ln_gain).astype(jnp.bfloat16)


def expert_hidden(rows, first, first_bias, second):
    pre = lax.dot_general(rows, first, (((1,), (1,)), ((), ())), preferred_element_type=jnp.float32)
    hidden = jax.nn.gelu(pre + first_bias.astype(jnp.float32), approximate=False).astype(
        jnp.bfloat16
    )
    return jnp.dot(hidden, second, preferred_element_type=jnp.float32)


def on_device(tokens, ln_gain, router, w_in, b_in, w_out, b_out, expert_choice, modality, slot):
    normed = layer_norm(tokens, ln_gain)
    logits = jnp.dot(normed, router, preferred_element_type=jnp.float32)
    logp = jax.nn.log_softmax(logits, axis=-1)
    probs = jnp.exp(logp)
    gate = jnp.take_along_axis(probs, expert_choice[:, None], axis=1)[:, 0]
    experts_all = router.shape[1]
    width = normed.shape[1]
    columns = experts_all * CAP
    target = jnp.where(slot >= 0, expert_choice * CAP + slot, -1)
    table = (target[:, None] == jnp.arange(columns, dtype=jnp.int32)[None, :]).astype(jnp.bfloat16)
    buffer = jnp.einsum("tk,td->kd", table, normed, preferred_element_type=jnp.float32).astype(
        jnp.bfloat16
    )
    received = lax.all_to_all(
        buffer.reshape(experts_all, CAP, width), EXPERT, split_axis=0, concat_axis=0, tiled=True
    )
    senders = lax.axis_size(EXPERT)
    local_count = w_in.shape[0]
    received = received.reshape(senders, local_count, CAP, width)
    rows = received[:, 0].reshape(senders * CAP, width)
    summed = expert_hidden(
        rows,
        lax.all_gather(w_in[0], "dp", axis=0, tiled=True),
        lax.all_gather(b_in[0], "dp", axis=0, tiled=True),
        lax.all_gather(w_out[0], "dp", axis=0, tiled=True),
    )
    results = [
        (summed + b_out[0].astype(jnp.float32)).astype(jnp.bfloat16).reshape(senders, CAP, width)
    ]
    outputs = jnp.stack(results, axis=1).reshape(experts_all, CAP, width)
    returned = lax.all_to_all(outputs, EXPERT, split_axis=0, concat_axis=0, tiled=True)
    fetched = jnp.dot(table, returned.reshape(columns, width), preferred_element_type=jnp.float32)
    moe_out = (gate[:, None] * fetched).astype(jnp.bfloat16)
    textual = (modality == 1).astype(jnp.float32)
    select = jnp.stack([1.0 - textual, textual], axis=0)
    entropy = -jnp.sum(probs * logp, axis=-1)
    prob_part = jnp.dot(select, probs, precision=lax.Precision.HIGHEST)
    ent_part = jnp.dot(select, entropy, precision=lax.Precision.HIGHEST)
    count_part = jnp.sum(select, axis=1)
    prob_sum, ent_sum, count = (
        by_axis(prob_part, DP_EXPERT),
        by_axis(ent_part, DP_EXPERT),
        by_axis(count_part, DP_EXPERT),
    )
    pbar = prob_sum / count[:, None]
    aux_losses = jnp.stack([ent_sum / count, jnp.sum(pbar * jnp.log(pbar), axis=1)], axis=1)
    return (moe_out, aux_losses)


def solution(mesh):
    finer = Mesh(
        mesh.devices.reshape(mesh.shape["dp"], 4, 4, 2), ("dp", "expert_0", "expert_1", "expert_2")
    )
    return jax.shard_map(
        on_device,
        mesh=finer,
        in_specs=(
            P(DP_EXPERT, None),
            P(),
            P(),
            P(EXPERT, "dp", None),
            P(EXPERT, "dp"),
            P(EXPERT, "dp", None),
            P(EXPERT, None),
            P(DP_EXPERT),
            P(DP_EXPERT),
            P(DP_EXPERT),
        ),
        out_specs=(P(DP_EXPERT, None), P()),
        check_vma=False,
    )
```

profile of v0, /device:TPU:1, one launch (start us, length us, event | category | flops | bytes accessed | tf_op | source)
XLA Modules:
  0.0 363.0 jit_solution(15232666370423474647)
XLA Ops:
  7.2 0.0 copy-start
  7.2 0.0 copy-start.4
  7.2 0.0 copy-start.1
  7.2 0.0 copy-start.2
  7.2 0.0 all-gather.6.cloned.1.call-start
  7.3 0.7 all-gather.6.cloned.1.call-update
  7.9 0.0 all-gather.8.cloned.1.call-start
  8.0 0.7 all-gather.8.cloned.1.call-update
  8.7 1.3 convert_reduce_fusion
  10.0 1.4 fusion.62
  11.4 0.7 compare_select_fusion
  12.1 2.9 convolution_convert_fusion
  15.0 8.6 %all-to-all-start = ((bf16[32,16,1280]{2,1,0:T(8,128)(2,1)}), bf16[32,16,1280]{2,1,0:T(8,128)(2,1)S(1)}, u32[]{:S(2)}, u32[]{:S(2)}) async-start(bf16[32,16,1280]{2,1,0:T(8,128)(2,1)} %bitcast.3), calls=%async_computation | async-start | bytes 2621440 | tf_op jit(solution)/shard_map/all_to_all | solution.py:46
  23.6 0.0 copy-done
  23.6 1.5 fusion.106
  25.2 0.0 copy-done.4
  25.2 25.4 %all-gather.1 = bf16[1,5120]{1,0:T(2,128)(2,1)S(1)} all-gather(bf16[1,640]{1,0:T(2,128)(2,1)S(1)} %copy-done.4), channel_id=3, replica_groups=mesh['dp'=8,'expert_0'=4,'expert_1'=4,'expert_2'=2] {'dp'}, dimensions={1}, use_global_device_ids=true | all-gather | bytes 11520 | tf_op jit(solution)/shard_map/all_gather | solution.py:56
  50.6 0.0 copy-done.1
  50.7 0.0 copy-done.2
  50.7 0.0 all-to-all-done
  50.7 101.4 %all-gather.6.cloned.1.call-done = bf16[1,5120,1280]{2,1,0:T(8,128)(2,1)} async-done(((bf16[1,640,1280]{2,1,0:T(8,128)(2,1)}), bf16[1,5120,1280]{2,1,0:T(8,128)(2,1)}) %all-gather.6.cloned.1.call-update) | async-done | bytes 13107216 | tf_op jit(solution)/shard_map/all_gather | solution.py:55
  152.1 31.7 %fusion.6.clone.8 = bf16[512,5120]{1,0:T(8,128)(2,1)} fusion(bf16[512,1280]{1,0:T(8,128)(2,1)S(1)} %bitcast.49, bf16[1,5120,1280]{2,1,0:T(8,128)(2,1)} %all-gather.6.cloned.1.call-done, f32[5120]{0:T(1024)S(1)} %bitcast.50), kind=kOutput, calls=%fused_computation.8.clone.clone.clone.clone.clone.clone.clone.1 | convolution fusion | flops 6883901440 | bytes 19681280 | tf_op jit(solution)/shard_map/dot_general | solution.py:25
  183.8 0.0 copy-start.3
  183.8 106.9 %all-gather.8.cloned.1.call-done = bf16[1,5120,1280]{2,1,0:T(8,128)(2,1)} async-done(((bf16[1,640,1280]{2,1,0:T(8,128)(2,1)}), bf16[1,5120,1280]{2,1,0:T(8,128)(2,1)}) %all-gather.8.cloned.1.call-update) | async-done | bytes 13107216 | tf_op jit(solution)/shard_map/all_gather | solution.py:57
  290.8 13.5 %fusion.54 = bf16[512,1280]{1,0:T(8,128)(2,1)} fusion(bf16[1,5120,1280]{2,1,0:T(8,128)(2,1)} %all-gather.8.cloned.1.call-done, f32[1280]{0:T(1024)S(1)} %convert_reduce_fusion.1, bf16[512,5120]{1,0:T(8,128)(2,1)} %fusion.6.clone.8), kind=kOutput, calls=%fused_computation.57 | convolution fusion | flops 6712197120 | bytes 19665920 | tf_op jit(solution)/shard_map/dot_general | solution.py:29
  304.2 7.7 %all-to-all-start.1 = ((bf16[32,16,1280]{2,1,0:T(8,128)(2,1)}), bf16[32,16,1280]{2,1,0:T(8,128)(2,1)S(1)}, u32[]{:S(2)}, u32[]{:S(2)}) async-start(bf16[32,16,1280]{2,1,0:T(8,128)(2,1)} %bitcast.8), calls=%async_computation.1 | async-start | bytes 2621440 | tf_op jit(solution)/shard_map/all_to_all | solution.py:63
  311.9 0.1 convolution_bitcast_fusion
  312.1 0.1 fusion.102
  312.2 0.1 fusion.67
  312.3 12.9 %all-reduce = (f32[2,32]{1,0:T(2,128)S(1)}, f32[2]{0:T(128)S(1)}, f32[2]{0:T(128)S(1)}) all-reduce(f32[2,32]{1,0:T(2,128)S(1)} %fusion.67, f32[2]{0:T(128)S(1)} %fusion.102, f32[2]{0:T(128)S(1)} %convolution_bitcast_fusion), channel_id=1, replica_groups=mesh['dp'=8,'expert_0'=4,'expert_1'=4,'expert_2'=2] {'dp'}, use_global_device_ids=true, to_apply=%region_14.15 | all-reduce | flops 68 | bytes 544 | tf_op jit(solution)/shard_map/psum | solution.py:14
  325.3 8.6 %all-reduce.2 = (f32[2,32]{1,0:T(2,128)S(1)}, f32[2]{0:T(128)S(1)}, f32[2]{0:T(128)S(1)}) all-reduce(f32[2,32]{1,0:T(2,128)S(1)} %get-tuple-element.8, f32[2]{0:T(128)S(1)} %get-tuple-element.9, f32[2]{0:T(128)S(1)} %get-tuple-element.10), channel_id=1, replica_groups=mesh['dp'=8,'expert_0'=4,'expert_1'=4,'expert_2'=2] {'expert_0'}, use_global_device_ids=true, to_apply=%region_15.16 | all-reduce | flops 68 | bytes 544 | tf_op jit(solution)/shard_map/psum | solution.py:14
  333.9 8.4 %all-reduce.1 = (f32[2,32]{1,0:T(2,128)S(1)}, f32[2]{0:T(128)S(1)}, f32[2]{0:T(128)S(1)}) all-reduce(f32[2,32]{1,0:T(2,128)S(1)} %get-tuple-element.14, f32[2]{0:T(128)S(1)} %get-tuple-element.15, f32[2]{0:T(128)S(1)} %get-tuple-element.16), channel_id=1, replica_groups=mesh['dp'=8,'expert_0'=4,'expert_1'=4,'expert_2'=2] {'expert_1'}, use_global_device_ids=true, to_apply=%region_16.17 | all-reduce | flops 68 | bytes 544 | tf_op jit(solution)/shard_map/psum | solution.py:14
  342.3 9.1 %all-reduce.3 = (f32[2,32]{1,0:T(2,128)S(1)}, f32[2]{0:T(128)S(1)}, f32[2]{0:T(128)S(1)}) all-reduce(f32[2,32]{1,0:T(2,128)S(1)} %get-tuple-element.11, f32[2]{0:T(128)S(1)} %get-tuple-element.12, f32[2]{0:T(128)S(1)} %get-tuple-element.13), channel_id=1, replica_groups=mesh['dp'=8,'expert_0'=4,'expert_1'=4,'expert_2'=2] {'expert_2'}, use_global_device_ids=true, to_apply=%region_17.18 | all-reduce | flops 68 | bytes 544 | tf_op jit(solution)/shard_map/psum | solution.py:14
  351.4 0.2 fusion.68
  351.6 0.7 copy.14
  352.3 2.4 gather_fusion
  354.7 0.0 copy-done.3
  354.7 0.0 all-to-all-done.1
  354.7 1.4 fusion.59
  (16 shorter events, 0.2 us)
Async XLA Ops:
  7.2 16.4 %copy-start = (bf16[1280,32]{0,1:T(8,128)(2,1)S(1)}, bf16[1280,32]{0,1:T(8,128)(2,1)}, u32[]{:S(2)}) copy-start(bf16[1280,32]{0,1:T(8,128)(2,1)} %param.12) | copy-start | bytes 245764
  7.2 18.0 %copy-start.4 = (bf16[1,640]{1,0:T(2,128)(2,1)S(1)}, bf16[1,640]{1,0:T(2,128)(2,1)}, u32[]{:S(2)}) copy-start(bf16[1,640]{1,0:T(2,128)(2,1)} %param.14) | copy-start | bytes 3844
  7.2 43.4 %copy-start.1 = (bf16[1,1280]{1,0:T(2,128)(2,1)S(1)}, bf16[1,1280]{1,0:T(2,128)(2,1)}, u32[]{:S(2)}) copy-start(bf16[1,1280]{1,0:T(2,128)(2,1)} %param.16) | copy-start | bytes 7684
  7.2 43.5 %copy-start.2 = (s32[256]{0:T(256)S(1)}, s32[256]{0:T(256)}, u32[]{:S(2)}) copy-start(s32[256]{0:T(256)} %param.18) | copy-start | bytes 3076
  7.2 144.9 %all-gather.6.cloned.1.call-start = ((), (), s32[]{:S(2)}) async-start(), calls=%async_computation.2 | async-start | bytes 14745600 | tf_op jit(solution)/shard_map/all_gather | solution.py:55
  7.9 282.8 %all-gather.8.cloned.1.call-start = ((), (), s32[]{:S(2)}) async-start(), calls=%async_computation.3 | async-start | bytes 14745600 | tf_op jit(solution)/shard_map/all_gather | solution.py:57
  15.0 35.7 %all-to-all-start = ((bf16[32,16,1280]{2,1,0:T(8,128)(2,1)}), bf16[32,16,1280]{2,1,0:T(8,128)(2,1)S(1)}, u32[]{:S(2)}, u32[]{:S(2)}) async-start(bf16[32,16,1280]{2,1,0:T(8,128)(2,1)} %bitcast.3), calls=%async_computation | async-start | bytes 2621440 | tf_op jit(solution)/shard_map/all_to_all | solution.py:46
  183.8 170.9 %copy-start.3 = (s32[256]{0:T(256)S(1)}, s32[256]{0:T(256)}, u32[]{:S(2)}) copy-start(s32[256]{0:T(256)} %param.17) | copy-start | bytes 3076
  304.2 50.5 %all-to-all-start.1 = ((bf16[32,16,1280]{2,1,0:T(8,128)(2,1)}), bf16[32,16,1280]{2,1,0:T(8,128)(2,1)S(1)}, u32[]{:S(2)}, u32[]{:S(2)}) async-start(bf16[32,16,1280]{2,1,0:T(8,128)(2,1)} %bitcast.8), calls=%async_computation.1 | async-start | bytes 2621440 | tf_op jit(solution)/shard_map/all_to_all | solution.py:63
Sparse Core Ops, SparseCore 0:
  9.8 142.2 all-gather.5
  153.9 136.8 all-gather.7
where the time goes:
time: 363 us
  waiting for transfers between devices  210 us (58%)
  blocking collectives  64.5 us (18%)
  matrix products  51.3 us (14%)
  starting transfers between devices  16.4 us (5%)
  between operations  14.2 us (4%)
  other arithmetic  3.85 us (1%)
    all_gather x1, waiting for transfers between devices, on_device(): lax.all_gather(w_out[0], 'dp', axis=0, tiled=True)  107 us
    all_gather x1, waiting for transfers between devices, on_device(): lax.all_gather(w_in[0], 'dp', axis=0, tiled=True)  101 us
    psum x4, blocking collectives, by_axis(): return functools.reduce(lax.psum, axes, x)  39.1 us
    dot_general x1, matrix products, expert_hidden(): lax.dot_general(rows, first, (((1,), (1,)), ((), ())), preferred_element_...  31.7 us
    all_gather x1, blocking collectives, on_device(): lax.all_gather(b_in[0], 'dp', axis=0, tiled=True)  25.4 us
    dot_general x1, matrix products, expert_hidden(): return jnp.dot(hidden, second, preferred_element_type=jnp.float32)  13.5 us
    all_to_all x1, starting transfers between devices, on_device(): lax.all_to_all(buffer.reshape(experts_all, CAP, width), EXPERT, split_axi...  8.58 us
    all_to_all x1, starting transfers between devices, on_device(): lax.all_to_all(outputs, EXPERT, split_axis=0, concat_axis=0, tiled=True)  7.7 us
  transfers between devices with their start and end apart: 4, of which 2 were waited for; matrix products, arithmetic and copies ran while one was open for 12% of the time, Pallas kernels for 0%

commit v1 on v0

--- a/solution.py
+++ b/solution.py
@@ -52,7 +52,9 @@
     rows = received[:, 0].reshape(senders * CAP, width)
     summed = expert_hidden(
         rows,
-        lax.all_gather(w_in[0], "dp", axis=0, tiled=True),
+        jnp.concatenate(
+            lax.all_to_all(jnp.stack([w_in[0]] * lax.axis_size("dp")), "dp", 0, 0), axis=0
+        ),
         lax.all_gather(b_in[0], "dp", axis=0, tiled=True),
         lax.all_gather(w_out[0], "dp", axis=0, tiled=True),
     )

time: 363 us -> 584 us (1.61)
  blocking collectives: 64.5 us -> 488 us
  waiting for transfers between devices: 210 us -> 0.69 us
  local copies, waits for them, and re-layouts: 3.06 us -> 10.1 us
    all_gather x1, blocking collectives: 25.4 us -> 418 us  [on_device(): lax.all_gather(b_in[0], 'dp', axis=0, tiled=True)]
    all_gather x1, waiting for transfers between devices: 107 us -> 0.01 us  [on_device(): lax.all_gather(w_out[0], 'dp', axis=0, tiled=True)]
    all_gather x1 -> x0, waiting for transfers between devices: 101 us -> none  [on_device(): lax.all_gather(w_in[0], 'dp', axis=0, tiled=True)]
    all_to_all x0 -> x1, blocking collectives: none -> 28.5 us  [on_device(): lax.all_to_all(buffer.reshape(experts_all, CAP, width), EXPERT, split_axi...]
    another operation x0 -> x1, local copies, waits for them, and re-layouts: none -> 7 us  [on_device(): jnp.stack([w_in[0]] * lax.axis_size('dp'))]
  transfers between devices with their start and end apart: 4 -> 3, of which waited for: 2 -> 0; matrix products, arithmetic and copies ran while one was open for 12% -> 6% of each run, Pallas kernels for 0% -> 0%
where the time goes in v1:
time: 584 us
  blocking collectives  488 us (84%)
  matrix products  49.2 us (8%)
  starting transfers between devices  17.8 us (3%)
  between operations  14.2 us (2%)
  local copies, waits for them, and re-layouts  10.1 us (2%)
    all_gather x1, blocking collectives, on_device(): lax.all_gather(b_in[0], 'dp', axis=0, tiled=True)  418 us
    psum x4, blocking collectives, by_axis(): return functools.reduce(lax.psum, axes, x)  41.2 us
    dot_general x1, matrix products, expert_hidden(): lax.dot_general(rows, first, (((1,), (1,)), ((), ())), preferred_element_...  31.8 us
    all_to_all x1, blocking collectives, on_device(): lax.all_to_all(buffer.reshape(experts_all, CAP, width), EXPERT, split_axi...  28.5 us
    dot_general x1, matrix products, expert_hidden(): return jnp.dot(hidden, second, preferred_element_type=jnp.float32)  13.5 us
  transfers between devices with their start and end apart: 3, of which 0 were waited for; matrix products, arithmetic and copies ran while one was open for 6% of the time, Pallas kernels for 0%

profile of v1, /device:TPU:1, one launch (start us, length us, event | category | flops | bytes accessed | tf_op | source)
XLA Modules:
  0.0 583.7 jit_solution(13066118093781119577)
XLA Ops:
  7.2 0.0 copy-start
  7.2 1.3 convert_reduce_fusion
  8.5 1.4 fusion.26
  9.9 0.7 compare_select_fusion
  10.6 1.9 convolution_convert_fusion
  12.5 28.5 %all_to_all.15 = bf16[32,16,1280]{2,1,0:T(8,128)(2,1)S(1)} all-to-all(bf16[32,16,1280]{2,1,0:T(8,128)(2,1)S(1)} %bitcast.43), channel_id=1, replica_groups=mesh['dp'=8,'expert_0'=4,'expert_1'=4,'expert_2'=2] {'expert_0','expert_..., dimensions={0} | all-to-all | bytes 2621440 | tf_op jit(solution)/shard_map/all_to_all | solution.py:46
  40.9 7.0 %stack.21 = bf16[8,640,1280]{2,1,0:T(8,128)(2,1)} broadcast(bf16[640,1280]{1,0:T(8,128)(2,1)} %bitcast.40), dimensions={1,2} | broadcast | bytes 14745600 | tf_op jit(solution)/shard_map/stack | solution.py:56
  47.9 0.0 copy-start.1
  47.9 0.0 copy-start.6
  47.9 0.0 copy-start.5
  47.9 0.0 copy-start.2
  47.9 0.0 copy-start.3
  48.0 8.3 %all-to-all-start.1 = ((bf16[8,640,1280]{2,1,0:T(8,128)(2,1)}), bf16[8,640,1280]{2,1,0:T(8,128)(2,1)}, u32[]{:S(2)}, u32[]{:S(2)}) async-start(bf16[8,640,1280]{2,1,0:T(8,128)(2,1)} %stack.21), calls=%async_computation.1 | async-start | bytes 26214400 | tf_op jit(solution)/shard_map/all_to_all | solution.py:56
  56.3 0.0 all-gather.4.cloned.1.call-start
  56.3 0.7 all-gather.4.cloned.1.call-update
  57.0 0.0 copy-done
  57.0 0.0 copy-done.1
  57.0 0.0 copy-done.6
  57.0 0.4 fusion.70
  57.6 0.0 copy-done.5
  57.6 418.2 %all-gather = bf16[1,5120]{1,0:T(2,128)(2,1)S(1)} all-gather(bf16[1,640]{1,0:T(2,128)(2,1)S(1)} %copy-done.5), channel_id=2, replica_groups=mesh['dp'=8,'expert_0'=4,'expert_1'=4,'expert_2'=2] {'dp'}, dimensions={1}, use_global_device_ids=true | all-gather | bytes 11520 | tf_op jit(solution)/shard_map/all_gather | solution.py:58
  475.8 0.0 copy-done.2
  475.9 0.0 copy-done.3
  475.9 0.0 all-to-all-done.1
  475.9 31.8 %fusion.4.clone.8 = bf16[512,5120]{1,0:T(8,128)(2,1)} fusion(bf16[512,1280]{1,0:T(8,128)(2,1)S(1)} %bitcast.42, bf16[5120,1280]{1,0:T(8,128)(2,1)} %bitcast.6, f32[5120]{0:T(1024)S(1)} %bitcast.44), kind=kOutput, calls=%fused_computation.6.clone.clone.clone.clone.clone.clone.clone.1 | convolution fusion | flops 6883901440 | bytes 19681280 | tf_op jit(solution)/shard_map/dot_general | solution.py:25
  507.7 0.0 copy-start.4
  507.7 0.0 all-gather.4.cloned.1.call-done
  507.7 13.5 %fusion.20 = bf16[512,1280]{1,0:T(8,128)(2,1)} fusion(bf16[1,5120,1280]{2,1,0:T(8,128)(2,1)} %all-gather.4.cloned.1.call-done, f32[1280]{0:T(1024)S(1)} %convert_reduce_fusion.1, bf16[512,5120]{1,0:T(8,128)(2,1)} %fusion.4.clone.8), kind=kOutput, calls=%fused_computation.29 | convolution fusion | flops 6712197120 | bytes 19665920 | tf_op jit(solution)/shard_map/dot_general | solution.py:29
  521.2 9.4 %all-to-all-start.2 = ((bf16[32,16,1280]{2,1,0:T(8,128)(2,1)}), bf16[32,16,1280]{2,1,0:T(8,128)(2,1)S(1)}, u32[]{:S(2)}, u32[]{:S(2)}) async-start(bf16[32,16,1280]{2,1,0:T(8,128)(2,1)} %bitcast.9), calls=%async_computation.2 | async-start | bytes 2621440 | tf_op jit(solution)/shard_map/all_to_all | solution.py:65
  530.6 0.1 convolution_bitcast_fusion
  530.7 0.1 fusion.66
  530.8 0.1 fusion.31
  531.0 14.9 %all-reduce = (f32[2,32]{1,0:T(2,128)S(1)}, f32[2]{0:T(128)S(1)}, f32[2]{0:T(128)S(1)}) all-reduce(f32[2,32]{1,0:T(2,128)S(1)} %fusion.31, f32[2]{0:T(128)S(1)} %fusion.66, f32[2]{0:T(128)S(1)} %convolution_bitcast_fusion), channel_id=1, replica_groups=mesh['dp'=8,'expert_0'=4,'expert_1'=4,'expert_2'=2] {'dp'}, use_global_device_ids=true, to_apply=%region_14.15 | all-reduce | flops 68 | bytes 544 | tf_op jit(solution)/shard_map/psum | solution.py:14
  545.9 8.7 %all-reduce.2 = (f32[2,32]{1,0:T(2,128)S(1)}, f32[2]{0:T(128)S(1)}, f32[2]{0:T(128)S(1)}) all-reduce(f32[2,32]{1,0:T(2,128)S(1)} %get-tuple-element.8, f32[2]{0:T(128)S(1)} %get-tuple-element.9, f32[2]{0:T(128)S(1)} %get-tuple-element.10), channel_id=1, replica_groups=mesh['dp'=8,'expert_0'=4,'expert_1'=4,'expert_2'=2] {'expert_0'}, use_global_device_ids=true, to_apply=%region_15.16 | all-reduce | flops 68 | bytes 544 | tf_op jit(solution)/shard_map/psum | solution.py:14
  554.6 8.4 %all-reduce.1 = (f32[2,32]{1,0:T(2,128)S(1)}, f32[2]{0:T(128)S(1)}, f32[2]{0:T(128)S(1)}) all-reduce(f32[2,32]{1,0:T(2,128)S(1)} %get-tuple-element.14, f32[2]{0:T(128)S(1)} %get-tuple-element.15, f32[2]{0:T(128)S(1)} %get-tuple-element.16), channel_id=1, replica_groups=mesh['dp'=8,'expert_0'=4,'expert_1'=4,'expert_2'=2] {'expert_1'}, use_global_device_ids=true, to_apply=%region_16.17 | all-reduce | flops 68 | bytes 544 | tf_op jit(solution)/shard_map/psum | solution.py:14
  563.0 9.1 %all-reduce.3 = (f32[2,32]{1,0:T(2,128)S(1)}, f32[2]{0:T(128)S(1)}, f32[2]{0:T(128)S(1)}) all-reduce(f32[2,32]{1,0:T(2,128)S(1)} %get-tuple-element.11, f32[2]{0:T(128)S(1)} %get-tuple-element.12, f32[2]{0:T(128)S(1)} %get-tuple-element.13), channel_id=1, replica_groups=mesh['dp'=8,'expert_0'=4,'expert_1'=4,'expert_2'=2] {'expert_2'}, use_global_device_ids=true, to_apply=%region_17.18 | all-reduce | flops 68 | bytes 544 | tf_op jit(solution)/shard_map/psum | solution.py:14
  572.1 0.2 fusion.32
  572.4 0.7 copy.14
  573.0 2.4 gather_fusion
  575.4 0.0 copy-done.4
  575.4 0.0 all-to-all-done.2
  575.5 1.4 fusion.23
  (16 shorter events, 0.2 us)
Async XLA Ops:
  7.2 49.9 %copy-start = (bf16[1280,32]{0,1:T(8,128)(2,1)S(1)}, bf16[1280,32]{0,1:T(8,128)(2,1)}, u32[]{:S(2)}) copy-start(bf16[1280,32]{0,1:T(8,128)(2,1)} %param.12) | copy-start | bytes 245764
  47.9 9.1 %copy-start.1 = (bf16[256,1280]{1,0:T(8,128)(2,1)S(1)}, bf16[256,1280]{1,0:T(8,128)(2,1)}, u32[]{:S(2)}) copy-start(bf16[256,1280]{1,0:T(8,128)(2,1)} %param.10) | copy-start | bytes 1966084
  47.9 9.1 %copy-start.6 = (f32[1280]{0:T(1024)S(1)}, f32[1280]{0:T(1024)}, u32[]{:S(2)}) copy-start(f32[1280]{0:T(1024)} %param.11) | copy-start | bytes 15364
  47.9 9.7 %copy-start.5 = (bf16[1,640]{1,0:T(2,128)(2,1)S(1)}, bf16[1,640]{1,0:T(2,128)(2,1)}, u32[]{:S(2)}) copy-start(bf16[1,640]{1,0:T(2,128)(2,1)} %param.14) | copy-start | bytes 3844
  47.9 427.9 %copy-start.2 = (bf16[1,1280]{1,0:T(2,128)(2,1)S(1)}, bf16[1,1280]{1,0:T(2,128)(2,1)}, u32[]{:S(2)}) copy-start(bf16[1,1280]{1,0:T(2,128)(2,1)} %param.16) | copy-start | bytes 7684
  47.9 427.9 %copy-start.3 = (s32[256]{0:T(256)S(1)}, s32[256]{0:T(256)}, u32[]{:S(2)}) copy-start(s32[256]{0:T(256)} %param.18) | copy-start | bytes 3076
  48.0 427.9 %all-to-all-start.1 = ((bf16[8,640,1280]{2,1,0:T(8,128)(2,1)}), bf16[8,640,1280]{2,1,0:T(8,128)(2,1)}, u32[]{:S(2)}, u32[]{:S(2)}) async-start(bf16[8,640,1280]{2,1,0:T(8,128)(2,1)} %stack.21), calls=%async_computation.1 | async-start | bytes 26214400 | tf_op jit(solution)/shard_map/all_to_all | solution.py:56
  56.3 451.4 %all-gather.4.cloned.1.call-start = ((), (), s32[]{:S(2)}) async-start(), calls=%async_computation.3 | async-start | bytes 14745600 | tf_op jit(solution)/shard_map/all_gather | solution.py:59
  507.7 67.8 %copy-start.4 = (s32[256]{0:T(256)S(1)}, s32[256]{0:T(256)}, u32[]{:S(2)}) copy-start(s32[256]{0:T(256)} %param.17) | copy-start | bytes 3076
  521.2 54.3 %all-to-all-start.2 = ((bf16[32,16,1280]{2,1,0:T(8,128)(2,1)}), bf16[32,16,1280]{2,1,0:T(8,128)(2,1)S(1)}, u32[]{:S(2)}, u32[]{:S(2)}) async-start(bf16[32,16,1280]{2,1,0:T(8,128)(2,1)} %bitcast.9), calls=%async_computation.2 | async-start | bytes 2621440 | tf_op jit(solution)/shard_map/all_to_all | solution.py:65
Sparse Core Ops, SparseCore 0:
  58.9 404.5 all-gather.3
